TPU v7x, 512 devices: a 8x2x16 block of a 8x8x16 slice. The times are simulated.
512 devices in a mesh: groups: 2 (over y), mp: 16 (over z), dp: 8 (over x), guide: 2 (over core).
Axes of the slice: x: 8, y: 2, z: 16, core: 2. Of those that a mesh axis runs over, the one named last changes fastest.
The devices are a block of a 8x8x16 slice.
Arguments:
- tokens: bfloat16 [768, 8192], P(('groups', 'mp'), ('dp', 'guide')), parts along dimension 0, may hold values from -6 to 6
- w_gate: bfloat16 [8192, 14336], P(('dp', 'guide'), 'mp'), may hold values from -0.0625 to 0.0625
- w_up: bfloat16 [8192, 14336], P(('dp', 'guide'), 'mp'), may hold values from -0.0625 to 0.0625
- w_down: bfloat16 [14336, 8192], P('mp', ('dp', 'guide')), may hold values from -0.046875 to 0.046875
Outputs:
- layer_output: bfloat16 [768, 8192], P(('groups', 'mp'), ('dp', 'guide')), parts along dimension 0
There are 2 independent parts, one for each index of `groups`. A program takes and returns all parts, laid end to end along the dimension named above; an argument that names none is the same for every part. Nothing has to cross between parts.
All inputs are finite; a program needn't handle non-finite values.
Results may differ from a plain program's by a relative error of at most 0.0049.
Values may be sent and summed in bfloat16 or wider, within the bound.
No kernel may reach another device: no remote copies, remote signals or barrier semaphores. Data moves between devices by JAX's collectives and lax.ppermute only.
A program may use at most 64 MiB of HBM per device.

v0:
```python
import jax
import jax.numpy as jnp
from jax import lax
from jax.sharding import PartitionSpec as P


def summed_on_arrival(tiles, axis):
    arrived = lax.all_to_all(tiles, axis, split_axis=0, concat_axis=0, tiled=True)
    total = arrived[0].astype(jnp.float32)
    for tile in arrived[1:]:
        total = total + tile.astype(jnp.float32)
    return total


def from_other_core(array):
    count = lax.axis_size("guide")
    return lax.ppermute(array, "guide", [(core, (core + 1) % count) for core in range(count)])


def per_device(tokens, w_gate, w_up, w_down):
    columns = w_gate.shape[1]
    rows, features = tokens.shape
    mp, dp, guide = (lax.axis_size(axis) for axis in ("mp", "dp", "guide"))
    core = lax.axis_index("guide")
    head = 2 * rows // 3
    tail = rows - head
    own_parity = lax.axis_index("mp") % guide == core
    other_tokens = from_other_core(tokens)
    both = jnp.stack([tokens, other_tokens])
    own_weights = lax.optimization_barrier(jnp.concatenate([w_gate, w_up], axis=1))
    other_weights = from_other_core(own_weights)
    other_w_down = from_other_core(w_down)
    owned = jnp.where(
        own_parity,
        both[:, :head],
        jnp.pad(both[:, head:], ((0, 0), (0, head - tail), (0, 0))),
    )
    blocks = lax.all_gather(owned.reshape(-1, features), "mp", axis=0, tiled=True)
    blocks = blocks.reshape(dp, guide, 2, head, features)
    heads = lax.dynamic_index_in_dim(blocks, core, 1, keepdims=False)
    tails = lax.dynamic_index_in_dim(blocks, 1 - core, 1, keepdims=False)[:, :, :tail]
    mine = jnp.concatenate([heads, tails], axis=2)
    chip_terms = jnp.dot(
        mine[:, 0].reshape(-1, features), own_weights, preferred_element_type=jnp.float32
    ) + jnp.dot(
        mine[:, 1].reshape(-1, features), other_weights, preferred_element_type=jnp.float32
    )
    summed = summed_on_arrival(chip_terms.astype(jnp.bfloat16).reshape(dp, rows, -1), "dp")
    hidden_share = (jax.nn.silu(summed[:, :columns]) * summed[:, columns:]).astype(jnp.bfloat16)
    copies = jnp.broadcast_to(hidden_share[None], (dp, *hidden_share.shape))
    hidden = lax.all_to_all(copies, "dp", 0, 0, tiled=True).reshape(dp * rows, columns)
    hidden, core = lax.optimization_barrier((hidden, core))
    halves = jnp.stack(
        [
            jnp.dot(hidden, w, preferred_element_type=jnp.float32)
            .astype(jnp.bfloat16)
            .reshape(dp, rows, -1)
            for w in (w_down, other_w_down)
        ],
        axis=1,
    )
    tiles = jnp.where(
        (jnp.arange(guide) == core)[None, :, None, None, None],
        halves[:, None, :, :head],
        jnp.pad(halves[:, None, :, head:], ((0, 0), (0, 0), (0, 0), (0, head - tail), (0, 0))),
    )
    output_rows = summed_on_arrival(tiles.reshape(mp, 2 * head, -1), "mp").astype(jnp.bfloat16)
    kept, received = output_rows[:head], from_other_core(output_rows[head:])
    return jnp.where(
        own_parity,
        jnp.concatenate([kept, received[:tail]], axis=0),
        jnp.concatenate([received, kept[:tail]], axis=0),
    )


def solution(mesh):
    placed = (
        P(("groups", "mp"), ("dp", "guide")),
        P(("dp", "guide"), "mp"),
        P(("dp", "guide"), "mp"),
        P("mp", ("dp", "guide")),
    )
    return jax.shard_map(
        per_device,
        mesh=mesh,
        in_specs=placed,
        out_specs=P(("groups", "mp"), ("dp", "guide")),
        check_vma=False,
    )
```

profile of v0, /device:TPU:80, one launch (start us, length us, event | category | flops | bytes accessed | tf_op | source)
XLA Modules:
  0.0 147.4 jit_solution(13465099907005168116)
XLA Ops:
  0.0 1.6 %pad_maximum_fusion = bf16[512,1792]{1,0:T(8,128)(2,1)S(1)} fusion(bf16[512,896]{1,0:T(8,128)(2,1)} %param.6, bf16[512,896]{1,0:T(8,128)(2,1)} %param.5), kind=kLoop, calls=%fused_computation.2 | loop fusion | flops 3670016 | bytes 3670016 | tf_op jit(solution)/shard_map/concatenate | solution.py:30
  1.6 2.0 %collective-permute-start.1 = (bf16[512,1792]{1,0:T(8,128)(2,1)S(1)}, bf16[512,1792]{1,0:T(8,128)(2,1)}, u32[]{:S(2)}, u32[]{:S(2)}) collective-permute-start(bf16[512,1792]{1,0:T(8,128)(2,1)S(1)} %pad_maximum_fusion), channel_id=1, source_target_pairs={{0,1},{1,0},{2,3},{3,2},{4,5},{5,4},{6,7},{7,6},{8,9},{9,8},{10,11... | collective-permute-start | bytes 5505032 | tf_op jit(solution)/shard_map/ppermute | solution.py:17
  3.6 2.4 %collective-permute-start = (bf16[24,512]{1,0:T(8,128)(2,1)S(1)}, bf16[24,512]{1,0:T(8,128)(2,1)S(1)}, u32[]{:S(2)}, u32[]{:S(2)}) collective-permute-start(bf16[24,512]{1,0:T(8,128)(2,1)S(1)} %copy-done.1), channel_id=1, source_target_pairs={{0,1},{1,0},{2,3},{3,2},{4,5},{5,4},{6,7},{7,6},{8,9},{9,8},{10,11... | collective-permute-start | bytes 73736 | tf_op jit(solution)/shard_map/ppermute | solution.py:17
  6.0 1.4 collective-permute-done
  7.5 70.8 %all_gather.3 = bf16[512,512]{1,0:T(8,128)(2,1)S(1)} all-gather(bf16[32,512]{1,0:T(8,128)(2,1)S(1)} %bitcast.48), channel_id=1, replica_groups=mesh['groups'=2,'mp'=16,'dp'=8,'guide'=2] {'mp'}, dimensions={0}, use_global_device_ids=true | all-gather | bytes 557056 | tf_op jit(solution)/shard_map/all_gather | solution.py:38
  78.4 0.5 fusion.12
  78.9 0.0 copy-start
  79.0 3.0 %fusion = bf16[192,1792]{1,0:T(8,128)(2,1)} fusion(f32[192,1792]{1,0:T(8,128)S(1)} %fusion.12, bf16[192,512]{1,0:T(8,128)(2,1)S(1)} %bitcast.46, bf16[512,1792]{1,0:T(8,128)(2,1)} %collective-permute-done.1), kind=kOutput, calls=%fused_computation.1 | convolution fusion | flops 353009664 | bytes 4096000 | tf_op jit(solution)/shard_map/dot_general | solution.py:45
  81.9 7.3 %all-to-all-start = ((bf16[8,24,1792]{2,1,0:T(8,128)(2,1)}), bf16[8,24,1792]{2,1,0:T(8,128)(2,1)S(1)}, u32[]{:S(2)}, u32[]{:S(2)}) async-start(bf16[8,24,1792]{2,1,0:T(8,128)(2,1)} %bitcast.8), calls=%async_computation | async-start | bytes 1376256 | tf_op jit(solution)/shard_map/all_to_all | solution.py:8
  89.2 2.0 %collective-permute-start.2 = (bf16[896,512]{1,0:T(8,128)(2,1)S(1)}, bf16[896,512]{1,0:T(8,128)(2,1)S(1)}, u32[]{:S(2)}, u32[]{:S(2)}) collective-permute-start(bf16[896,512]{1,0:T(8,128)(2,1)S(1)} %copy-done), channel_id=1, source_target_pairs={{0,1},{1,0},{2,3},{3,2},{4,5},{5,4},{6,7},{7,6},{8,9},{9,8},{10,11... | collective-permute-start | bytes 2752520 | tf_op jit(solution)/shard_map/ppermute | solution.py:17
  91.2 13.1 %all-to-all-done = bf16[8,24,1792]{2,1,0:T(8,128)(2,1)S(1)} async-done(((bf16[8,24,1792]{2,1,0:T(8,128)(2,1)}), bf16[8,24,1792]{2,1,0:T(8,128)(2,1)S(1)}, u32[]{:S(2)}, u32[]{:S(2)}) %all-to-all-start) | async-done | bytes 688160 | tf_op jit(solution)/shard_map/all_to_all | solution.py:8
  104.3 0.1 add_bitcast_fusion
  104.5 13.8 %all_to_all.15 = bf16[8,24,896]{2,1,0:T(8,128)(2,1)S(1)} all-to-all(bf16[8,24,896]{2,1,0:T(8,128)(2,1)S(1)} %broadcast_in_dim.45), channel_id=1, replica_groups=mesh['groups'=2,'mp'=16,'dp'=8,'guide'=2] {'dp'}, dimensions={0} | all-to-all | bytes 688128 | tf_op jit(solution)/shard_map/all_to_all | solution.py:51
  118.2 0.4 convolution_convert_fusion.1
  118.6 0.4 convolution_convert_fusion
  119.2 0.1 broadcast_in_dim.47
  119.2 0.1 broadcast_in_dim.53
  119.3 0.1 broadcast_in_dim.49
  119.4 0.1 broadcast_select_fusion
  119.5 24.1 %all_to_all.16 = bf16[16,32,512]{2,1,0:T(8,128)(2,1)S(1)} all-to-all(bf16[16,32,512]{2,1,0:T(8,128)(2,1)S(1)} %broadcast_select_fusion), channel_id=1, replica_groups=mesh['groups'=2,'mp'=16,'dp'=8,'guide'=2] {'mp'}, dimensions={0} | all-to-all | bytes 1048576 | tf_op jit(solution)/shard_map/all_to_all | solution.py:8
  143.6 0.1 fusion.7
  143.6 2.0 %collective-permute-start.3 = (bf16[16,512]{1,0:T(8,128)(2,1)S(1)}, bf16[16,512]{1,0:T(8,128)(2,1)S(1)}, u32[]{:S(2)}, u32[]{:S(2)}) collective-permute-start(bf16[16,512]{1,0:T(8,128)(2,1)S(1)} %get-tuple-element.14), channel_id=1, source_target_pairs={{0,1},{1,0},{2,3},{3,2},{4,5},{5,4},{6,7},{7,6},{8,9},{9,8},{10,11... | collective-permute-start | bytes 49160 | tf_op jit(solution)/shard_map/ppermute | solution.py:17
  145.6 1.1 collective-permute-done.3
  146.8 0.6 maximum_select_fusion
  (21 shorter events, 0.3 us)
Async XLA Ops:
  0.0 3.6 %copy-start.1 = (bf16[24,512]{1,0:T(8,128)(2,1)S(1)}, bf16[24,512]{1,0:T(8,128)(2,1)}, u32[]{:S(2)}) copy-start(bf16[24,512]{1,0:T(8,128)(2,1)} %param.4) | copy-start | bytes 73732
  1.6 77.3 %collective-permute-start.1 = (bf16[512,1792]{1,0:T(8,128)(2,1)S(1)}, bf16[512,1792]{1,0:T(8,128)(2,1)}, u32[]{:S(2)}, u32[]{:S(2)}) collective-permute-start(bf16[512,1792]{1,0:T(8,128)(2,1)S(1)} %pad_maximum_fusion), channel_id=1, source_target_pairs={{0,1},{1,0},{2,3},{3,2},{4,5},{5,4},{6,7},{7,6},{8,9},{9,8},{10,11... | collective-permute-start | bytes 5505032 | tf_op jit(solution)/shard_map/ppermute | solution.py:17
  3.6 3.9 %collective-permute-start = (bf16[24,512]{1,0:T(8,128)(2,1)S(1)}, bf16[24,512]{1,0:T(8,128)(2,1)S(1)}, u32[]{:S(2)}, u32[]{:S(2)}) collective-permute-start(bf16[24,512]{1,0:T(8,128)(2,1)S(1)} %copy-done.1), channel_id=1, source_target_pairs={{0,1},{1,0},{2,3},{3,2},{4,5},{5,4},{6,7},{7,6},{8,9},{9,8},{10,11... | collective-permute-start | bytes 73736 | tf_op jit(solution)/shard_map/ppermute | solution.py:17
  78.9 10.3 %copy-start = (bf16[896,512]{1,0:T(8,128)(2,1)S(1)}, bf16[896,512]{1,0:T(8,128)(2,1)}, u32[]{:S(2)}) copy-start(bf16[896,512]{1,0:T(8,128)(2,1)} %param.7) | copy-start | bytes 2752516
  81.9 22.4 %all-to-all-start = ((bf16[8,24,1792]{2,1,0:T(8,128)(2,1)}), bf16[8,24,1792]{2,1,0:T(8,128)(2,1)S(1)}, u32[]{:S(2)}, u32[]{:S(2)}) async-start(bf16[8,24,1792]{2,1,0:T(8,128)(2,1)} %bitcast.8), calls=%async_computation | async-start | bytes 1376256 | tf_op jit(solution)/shard_map/all_to_all | solution.py:8
  89.2 29.4 %collective-permute-start.2 = (bf16[896,512]{1,0:T(8,128)(2,1)S(1)}, bf16[896,512]{1,0:T(8,128)(2,1)S(1)}, u32[]{:S(2)}, u32[]{:S(2)}) collective-permute-start(bf16[896,512]{1,0:T(8,128)(2,1)S(1)} %copy-done), channel_id=1, source_target_pairs={{0,1},{1,0},{2,3},{3,2},{4,5},{5,4},{6,7},{7,6},{8,9},{9,8},{10,11... | collective-permute-start | bytes 2752520 | tf_op jit(solution)/shard_map/ppermute | solution.py:17
  143.6 3.1 %collective-permute-start.3 = (bf16[16,512]{1,0:T(8,128)(2,1)S(1)}, bf16[16,512]{1,0:T(8,128)(2,1)S(1)}, u32[]{:S(2)}, u32[]{:S(2)}) collective-permute-start(bf16[16,512]{1,0:T(8,128)(2,1)S(1)} %get-tuple-element.14), channel_id=1, source_target_pairs={{0,1},{1,0},{2,3},{3,2},{4,5},{5,4},{6,7},{7,6},{8,9},{9,8},{10,11... | collective-permute-start | bytes 49160 | tf_op jit(solution)/shard_map/ppermute | solution.py:17
where the time goes:
time: 149 us; the launch traced here: 147 us
  blocking collectives  109 us (73%)
  waiting for transfers between devices  15.7 us (11%)
  starting transfers between devices  15.6 us (10%)
  matrix products  4.21 us (3%)
  other arithmetic  2.62 us (2%)
    all_gather x1, blocking collectives, per_device(): lax.all_gather(owned.reshape(-1, features), 'mp', axis=0, tiled=True)  70.8 us
    all_to_all x1, blocking collectives, summed_on_arrival(): lax.all_to_all(tiles, axis, split_axis=0, concat_axis=0, tiled=True)  24.1 us
    all_to_all x1, blocking collectives, per_device(): lax.all_to_all(copies, 'dp', 0, 0, tiled=True).reshape(dp * rows, columns)  13.8 us
    all_to_all x1, waiting for transfers between devices, summed_on_arrival(): lax.all_to_all(tiles, axis, split_axis=0, concat_axis=0, tiled=True)  13.1 us
    ppermute x4, starting transfers between devices, from_other_core(): lax.ppermute(array, 'guide', [(core, (core + 1) % count) for core in rang...  8.29 us
    all_to_all x1, starting transfers between devices, summed_on_arrival(): lax.all_to_all(tiles, axis, split_axis=0, concat_axis=0, tiled=True)  7.32 us
  transfers between devices with their start and end apart: 5, of which 3 were waited for; matrix products, arithmetic and copies ran while one was open for 1% of the time, Pallas kernels for 0%

commit v1 on v0

--- a/solution.py
+++ b/solution.py
@@ -27,8 +27,8 @@
     own_parity = lax.axis_index("mp") % guide == core
     other_tokens = from_other_core(tokens)
     both = jnp.stack([tokens, other_tokens])
-    own_weights = lax.optimization_barrier(jnp.concatenate([w_gate, w_up], axis=1))
-    other_weights = from_other_core(own_weights)
+    other_gate = from_other_core(w_gate)
+    other_up = from_other_core(w_up)
     other_w_down = from_other_core(w_down)
     owned = jnp.where(
         own_parity,
@@ -40,12 +40,19 @@
     heads = lax.dynamic_index_in_dim(blocks, core, 1, keepdims=False)
     tails = lax.dynamic_index_in_dim(blocks, 1 - core, 1, keepdims=False)[:, :, :tail]
     mine = jnp.concatenate([heads, tails], axis=2)
-    chip_terms = jnp.dot(
-        mine[:, 0].reshape(-1, features), own_weights, preferred_element_type=jnp.float32
-    ) + jnp.dot(
-        mine[:, 1].reshape(-1, features), other_weights, preferred_element_type=jnp.float32
+    own_rows, other_rows = (mine[:, half].reshape(-1, features) for half in range(2))
+    other_terms = [
+        jnp.dot(other_rows, w, preferred_element_type=jnp.float32) for w in (other_gate, other_up)
+    ]
+    own_rows, other_terms = lax.optimization_barrier((own_rows, other_terms))
+    chip_terms = jnp.concatenate(
+        [
+            (terms + jnp.dot(own_rows, w, preferred_element_type=jnp.float32)).astype(jnp.bfloat16)
+            for terms, w in zip(other_terms, (w_gate, w_up))
+        ],
+        axis=1,
     )
-    summed = summed_on_arrival(chip_terms.astype(jnp.bfloat16).reshape(dp, rows, -1), "dp")
+    summed = summed_on_arrival(chip_terms.reshape(dp, rows, -1), "dp")
     hidden_share = (jax.nn.silu(summed[:, :columns]) * summed[:, columns:]).astype(jnp.bfloat16)
     copies = jnp.broadcast_to(hidden_share[None], (dp, *hidden_share.shape))
     hidden = lax.all_to_all(copies, "dp", 0, 0, tiled=True).reshape(dp * rows, columns)

time: 149 us -> 150 us (level)
  starting transfers between devices: 15.6 us -> 17.7 us
  matrix products: 4.21 us -> 2.24 us
    dot_general x2 -> x4, matrix products: 3.49 us -> 1.51 us  [the longest x2 0.76 us: per_device(): jnp.dot(other_rows, w, preferred_element_type=jnp.float32)]
    ppermute x4 -> x5, starting transfers between devices: 8.29 us -> 10.2 us  [from_other_core(): lax.ppermute(array, 'guide', [(core, (core + 1) % count) for core in rang...]
  transfers between devices with their start and end apart: 5 -> 6, of which waited for: 3 -> 3; matrix products, arithmetic and copies ran while one was open for 1% -> 1% of each run, Pallas kernels for 0% -> 0%
where the time goes in v1:
time: 150 us; the launch traced here: 148 us
  blocking collectives  109 us (73%)
  starting transfers between devices  17.7 us (12%)
  waiting for transfers between devices  15.6 us (10%)
  other arithmetic  2.77 us (2%)
  matrix products  2.24 us (1%)
    all_gather x1, blocking collectives, per_device(): lax.all_gather(owned.reshape(-1, features), 'mp', axis=0, tiled=True)  70.9 us
    all_to_all x1, blocking collectives, summed_on_arrival(): lax.all_to_all(tiles, axis, split_axis=0, concat_axis=0, tiled=True)  24 us
    all_to_all x1, blocking collectives, per_device(): lax.all_to_all(copies, 'dp', 0, 0, tiled=True).reshape(dp * rows, columns)  13.8 us
    all_to_all x1, waiting for transfers between devices, summed_on_arrival(): lax.all_to_all(tiles, axis, split_axis=0, concat_axis=0, tiled=True)  13.1 us
    ppermute x5, starting transfers between devices, from_other_core(): lax.ppermute(array, 'guide', [(core, (core + 1) % count) for core in rang...  10.2 us
    all_to_all x1, starting transfers between devices, summed_on_arrival(): lax.all_to_all(tiles, axis, split_axis=0, concat_axis=0, tiled=True)  7.46 us
  transfers between devices with their start and end apart: 6, of which 3 were waited for; matrix products, arithmetic and copies ran while one was open for 1% of the time, Pallas kernels for 0%

profile of v1, /device:TPU:80, one launch (start us, length us, event | category | flops | bytes accessed | tf_op | source)
XLA Modules:
  0.0 148.5 jit_solution(13023318575016534458)
XLA Ops:
  0.0 1.9 %collective-permute-start.1 = (bf16[512,896]{1,0:T(8,128)(2,1)}, bf16[512,896]{1,0:T(8,128)(2,1)S(1)}, u32[]{:S(2)}, u32[]{:S(2)}) collective-permute-start(bf16[512,896]{1,0:T(8,128)(2,1)} %param.5), channel_id=1, source_target_pairs={{0,1},{1,0},{2,3},{3,2},{4,5},{5,4},{6,7},{7,6},{8,9},{9,8},{10,11... | collective-permute-start | bytes 2752520 | tf_op jit(solution)/shard_map/ppermute | solution.py:17
  1.9 2.4 %collective-permute-start.2 = (bf16[512,896]{1,0:T(8,128)(2,1)}, bf16[512,896]{1,0:T(8,128)(2,1)S(1)}, u32[]{:S(2)}, u32[]{:S(2)}) collective-permute-start(bf16[512,896]{1,0:T(8,128)(2,1)} %param.6), channel_id=1, source_target_pairs={{0,1},{1,0},{2,3},{3,2},{4,5},{5,4},{6,7},{7,6},{8,9},{9,8},{10,11... | collective-permute-start | bytes 2752520 | tf_op jit(solution)/shard_map/ppermute | solution.py:17
  4.4 2.0 %collective-permute-start = (bf16[24,512]{1,0:T(8,128)(2,1)}, bf16[24,512]{1,0:T(8,128)(2,1)S(1)}, u32[]{:S(2)}, u32[]{:S(2)}) collective-permute-start(bf16[24,512]{1,0:T(8,128)(2,1)} %param.4), channel_id=1, source_target_pairs={{0,1},{1,0},{2,3},{3,2},{4,5},{5,4},{6,7},{7,6},{8,9},{9,8},{10,11... | collective-permute-start | bytes 73736 | tf_op jit(solution)/shard_map/ppermute | solution.py:17
  6.4 1.4 collective-permute-done
  7.7 0.7 fusion.8
  8.5 70.9 %all_gather.3 = bf16[512,512]{1,0:T(8,128)(2,1)S(1)} all-gather(bf16[32,512]{1,0:T(8,128)(2,1)S(1)} %bitcast.54), channel_id=1, replica_groups=mesh['groups'=2,'mp'=16,'dp'=8,'guide'=2] {'mp'}, dimensions={0}, use_global_device_ids=true | all-gather | bytes 557056 | tf_op jit(solution)/shard_map/all_gather | solution.py:38
  79.4 0.4 fusion.11
  79.8 0.4 fusion.12
  80.2 0.8 copy-done
  81.0 0.4 fusion.14
  81.5 0.4 fusion.13
  81.9 0.1 add_convert_fusion
  82.0 0.9 pad_maximum_fusion
  82.9 7.5 %all-to-all-start = ((bf16[8,24,1792]{2,1,0:T(8,128)(2,1)}), bf16[8,24,1792]{2,1,0:T(8,128)(2,1)S(1)}, u32[]{:S(2)}, u32[]{:S(2)}) async-start(bf16[8,24,1792]{2,1,0:T(8,128)(2,1)} %bitcast.8), calls=%async_computation | async-start | bytes 1376256 | tf_op jit(solution)/shard_map/all_to_all | solution.py:8
  90.4 2.0 %collective-permute-start.3 = (bf16[896,512]{1,0:T(8,128)(2,1)S(1)}, bf16[896,512]{1,0:T(8,128)(2,1)S(1)}, u32[]{:S(2)}, u32[]{:S(2)}) collective-permute-start(bf16[896,512]{1,0:T(8,128)(2,1)S(1)} %copy-done.2), channel_id=1, source_target_pairs={{0,1},{1,0},{2,3},{3,2},{4,5},{5,4},{6,7},{7,6},{8,9},{9,8},{10,11... | collective-permute-start | bytes 2752520 | tf_op jit(solution)/shard_map/ppermute | solution.py:17
  92.3 13.1 %all-to-all-done = bf16[8,24,1792]{2,1,0:T(8,128)(2,1)S(1)} async-done(((bf16[8,24,1792]{2,1,0:T(8,128)(2,1)}), bf16[8,24,1792]{2,1,0:T(8,128)(2,1)S(1)}, u32[]{:S(2)}, u32[]{:S(2)}) %all-to-all-start) | async-done | bytes 688160 | tf_op jit(solution)/shard_map/all_to_all | solution.py:8
  105.6 13.8 %all_to_all.15 = bf16[8,24,896]{2,1,0:T(8,128)(2,1)S(1)} all-to-all(bf16[8,24,896]{2,1,0:T(8,128)(2,1)S(1)} %broadcast_in_dim.45), channel_id=1, replica_groups=mesh['groups'=2,'mp'=16,'dp'=8,'guide'=2] {'dp'}, dimensions={0} | all-to-all | bytes 688128 | tf_op jit(solution)/shard_map/all_to_all | solution.py:58
  119.4 0.4 convolution_convert_fusion.1
  119.8 0.4 convolution_convert_fusion
  120.5 0.1 broadcast_select_fusion
  120.6 24.0 %all_to_all.16 = bf16[16,32,512]{2,1,0:T(8,128)(2,1)S(1)} all-to-all(bf16[16,32,512]{2,1,0:T(8,128)(2,1)S(1)} %broadcast_select_fusion), channel_id=1, replica_groups=mesh['groups'=2,'mp'=16,'dp'=8,'guide'=2] {'mp'}, dimensions={0} | all-to-all | bytes 1048576 | tf_op jit(solution)/shard_map/all_to_all | solution.py:8
  144.7 2.0 %collective-permute-start.4 = (bf16[16,512]{1,0:T(8,128)(2,1)S(1)}, bf16[16,512]{1,0:T(8,128)(2,1)S(1)}, u32[]{:S(2)}, u32[]{:S(2)}) collective-permute-start(bf16[16,512]{1,0:T(8,128)(2,1)S(1)} %get-tuple-element.20), channel_id=1, source_target_pairs={{0,1},{1,0},{2,3},{3,2},{4,5},{5,4},{6,7},{7,6},{8,9},{9,8},{10,11... | collective-permute-start | bytes 49160 | tf_op jit(solution)/shard_map/ppermute | solution.py:17
  146.7 1.1 collective-permute-done.4
  147.9 0.6 maximum_select_fusion
  (28 shorter events, 0.7 us)
Async XLA Ops:
  0.0 79.4 %collective-permute-start.1 = (bf16[512,896]{1,0:T(8,128)(2,1)}, bf16[512,896]{1,0:T(8,128)(2,1)S(1)}, u32[]{:S(2)}, u32[]{:S(2)}) collective-permute-start(bf16[512,896]{1,0:T(8,128)(2,1)} %param.5), channel_id=1, source_target_pairs={{0,1},{1,0},{2,3},{3,2},{4,5},{5,4},{6,7},{7,6},{8,9},{9,8},{10,11... | collective-permute-start | bytes 2752520 | tf_op jit(solution)/shard_map/ppermute | solution.py:17
  1.9 77.9 %collective-permute-start.2 = (bf16[512,896]{1,0:T(8,128)(2,1)}, bf16[512,896]{1,0:T(8,128)(2,1)S(1)}, u32[]{:S(2)}, u32[]{:S(2)}) collective-permute-start(bf16[512,896]{1,0:T(8,128)(2,1)} %param.6), channel_id=1, source_target_pairs={{0,1},{1,0},{2,3},{3,2},{4,5},{5,4},{6,7},{7,6},{8,9},{9,8},{10,11... | collective-permute-start | bytes 2752520 | tf_op jit(solution)/shard_map/ppermute | solution.py:17
  4.4 3.3 %collective-permute-start = (bf16[24,512]{1,0:T(8,128)(2,1)}, bf16[24,512]{1,0:T(8,128)(2,1)S(1)}, u32[]{:S(2)}, u32[]{:S(2)}) collective-permute-start(bf16[24,512]{1,0:T(8,128)(2,1)} %param.4), channel_id=1, source_target_pairs={{0,1},{1,0},{2,3},{3,2},{4,5},{5,4},{6,7},{7,6},{8,9},{9,8},{10,11... | collective-permute-start | bytes 73736 | tf_op jit(solution)/shard_map/ppermute | solution.py:17
  79.8 1.2 copy-start
  80.2 1.3 copy-start.1
  82.9 7.5 %copy-start.2 = (bf16[896,512]{1,0:T(8,128)(2,1)S(1)}, bf16[896,512]{1,0:T(8,128)(2,1)}, u32[]{:S(2)}) copy-start(bf16[896,512]{1,0:T(8,128)(2,1)} %param.7) | copy-start | bytes 2752516
  82.9 22.5 %all-to-all-start = ((bf16[8,24,1792]{2,1,0:T(8,128)(2,1)}), bf16[8,24,1792]{2,1,0:T(8,128)(2,1)S(1)}, u32[]{:S(2)}, u32[]{:S(2)}) async-start(bf16[8,24,1792]{2,1,0:T(8,128)(2,1)} %bitcast.8), calls=%async_computation | async-start | bytes 1376256 | tf_op jit(solution)/shard_map/all_to_all | solution.py:8
  90.4 29.4 %collective-permute-start.3 = (bf16[896,512]{1,0:T(8,128)(2,1)S(1)}, bf16[896,512]{1,0:T(8,128)(2,1)S(1)}, u32[]{:S(2)}, u32[]{:S(2)}) collective-permute-start(bf16[896,512]{1,0:T(8,128)(2,1)S(1)} %copy-done.2), channel_id=1, source_target_pairs={{0,1},{1,0},{2,3},{3,2},{4,5},{5,4},{6,7},{7,6},{8,9},{9,8},{10,11... | collective-permute-start | bytes 2752520 | tf_op jit(solution)/shard_map/ppermute | solution.py:17
  144.7 3.1 %collective-permute-start.4 = (bf16[16,512]{1,0:T(8,128)(2,1)S(1)}, bf16[16,512]{1,0:T(8,128)(2,1)S(1)}, u32[]{:S(2)}, u32[]{:S(2)}) collective-permute-start(bf16[16,512]{1,0:T(8,128)(2,1)S(1)} %get-tuple-element.20), channel_id=1, source_target_pairs={{0,1},{1,0},{2,3},{3,2},{4,5},{5,4},{6,7},{7,6},{8,9},{9,8},{10,11... | collective-permute-start | bytes 49160 | tf_op jit(solution)/shard_map/ppermute | solution.py:17

commit v2 on v0

--- a/solution.py
+++ b/solution.py
@@ -59,10 +59,10 @@
         ],
         axis=1,
     )
-    tiles = jnp.where(
-        (jnp.arange(guide) == core)[None, :, None, None, None],
-        halves[:, None, :, :head],
-        jnp.pad(halves[:, None, :, head:], ((0, 0), (0, 0), (0, 0), (0, head - tail), (0, 0))),
+    heads = halves[:, :, :head]
+    tails = jnp.pad(halves[:, :, head:], ((0, 0), (0, 0), (0, head - tail), (0, 0)))
+    tiles = jnp.stack(
+        [jnp.where(core == parity, heads, tails) for parity in range(guide)], axis=1
     )
     output_rows = summed_on_arrival(tiles.reshape(mp, 2 * head, -1), "mp").astype(jnp.bfloat16)
     kept, received = output_rows[:head], from_other_core(output_rows[head:])

time: 149 us -> 149 us (level)
  no operation moved by 1% of the time
where the time goes in v2:
time: 149 us; the launch traced here: 147 us
  blocking collectives  109 us (73%)
  waiting for transfers between devices  15.7 us (11%)
  starting transfers between devices  15.6 us (10%)
  matrix products  4.22 us (3%)
  other arithmetic  2.61 us (2%)
    all_gather x1, blocking collectives, per_device(): lax.all_gather(owned.reshape(-1, features), 'mp', axis=0, tiled=True)  70.8 us
    all_to_all x1, blocking collectives, summed_on_arrival(): lax.all_to_all(tiles, axis, split_axis=0, concat_axis=0, tiled=True)  24.1 us
    all_to_all x1, blocking collectives, per_device(): lax.all_to_all(copies, 'dp', 0, 0, tiled=True).reshape(dp * rows, columns)  13.8 us
    all_to_all x1, waiting for transfers between devices, summed_on_arrival(): lax.all_to_all(tiles, axis, split_axis=0, concat_axis=0, tiled=True)  13.1 us
    ppermute x4, starting transfers between devices, from_other_core(): lax.ppermute(array, 'guide', [(core, (core + 1) % count) for core in rang...  8.29 us
    all_to_all x1, starting transfers between devices, summed_on_arrival(): lax.all_to_all(tiles, axis, split_axis=0, concat_axis=0, tiled=True)  7.32 us
  transfers between devices with their start and end apart: 5, of which 3 were waited for; matrix products, arithmetic and copies ran while one was open for 1% of the time, Pallas kernels for 0%

profile of v2, /device:TPU:80, one launch (start us, length us, event | category | flops | bytes accessed | tf_op | source)
XLA Modules:
  0.0 147.1 jit_solution(13608820078453039188)
XLA Ops:
  0.0 1.6 %pad_maximum_fusion = bf16[512,1792]{1,0:T(8,128)(2,1)S(1)} fusion(bf16[512,896]{1,0:T(8,128)(2,1)} %param.6, bf16[512,896]{1,0:T(8,128)(2,1)} %param.5), kind=kLoop, calls=%fused_computation.2 | loop fusion | flops 3670016 | bytes 3670016 | tf_op jit(solution)/shard_map/concatenate | solution.py:30
  1.6 2.0 %collective-permute-start.1 = (bf16[512,1792]{1,0:T(8,128)(2,1)S(1)}, bf16[512,1792]{1,0:T(8,128)(2,1)}, u32[]{:S(2)}, u32[]{:S(2)}) collective-permute-start(bf16[512,1792]{1,0:T(8,128)(2,1)S(1)} %pad_maximum_fusion), channel_id=1, source_target_pairs={{0,1},{1,0},{2,3},{3,2},{4,5},{5,4},{6,7},{7,6},{8,9},{9,8},{10,11... | collective-permute-start | bytes 5505032 | tf_op jit(solution)/shard_map/ppermute | solution.py:17
  3.6 2.4 %collective-permute-start = (bf16[24,512]{1,0:T(8,128)(2,1)S(1)}, bf16[24,512]{1,0:T(8,128)(2,1)S(1)}, u32[]{:S(2)}, u32[]{:S(2)}) collective-permute-start(bf16[24,512]{1,0:T(8,128)(2,1)S(1)} %copy-done.1), channel_id=1, source_target_pairs={{0,1},{1,0},{2,3},{3,2},{4,5},{5,4},{6,7},{7,6},{8,9},{9,8},{10,11... | collective-permute-start | bytes 73736 | tf_op jit(solution)/shard_map/ppermute | solution.py:17
  6.0 1.4 collective-permute-done
  7.5 70.8 %all_gather.3 = bf16[512,512]{1,0:T(8,128)(2,1)S(1)} all-gather(bf16[32,512]{1,0:T(8,128)(2,1)S(1)} %bitcast.44), channel_id=1, replica_groups=mesh['groups'=2,'mp'=16,'dp'=8,'guide'=2] {'mp'}, dimensions={0}, use_global_device_ids=true | all-gather | bytes 557056 | tf_op jit(solution)/shard_map/all_gather | solution.py:38
  78.4 0.5 fusion.14
  78.9 0.0 collective-permute-done.1
  78.9 0.0 copy-start
  79.0 3.0 %fusion = bf16[192,1792]{1,0:T(8,128)(2,1)} fusion(f32[192,1792]{1,0:T(8,128)S(1)} %fusion.14, bf16[192,512]{1,0:T(8,128)(2,1)S(1)} %bitcast.40, bf16[512,1792]{1,0:T(8,128)(2,1)} %collective-permute-done.1), kind=kOutput, calls=%fused_computation.1 | convolution fusion | flops 353009664 | bytes 4096000 | tf_op jit(solution)/shard_map/dot_general | solution.py:45
  81.9 7.3 %all-to-all-start = ((bf16[8,24,1792]{2,1,0:T(8,128)(2,1)}), bf16[8,24,1792]{2,1,0:T(8,128)(2,1)S(1)}, u32[]{:S(2)}, u32[]{:S(2)}) async-start(bf16[8,24,1792]{2,1,0:T(8,128)(2,1)} %bitcast.8), calls=%async_computation | async-start | bytes 1376256 | tf_op jit(solution)/shard_map/all_to_all | solution.py:8
  89.2 2.0 %collective-permute-start.2 = (bf16[896,512]{1,0:T(8,128)(2,1)S(1)}, bf16[896,512]{1,0:T(8,128)(2,1)S(1)}, u32[]{:S(2)}, u32[]{:S(2)}) collective-permute-start(bf16[896,512]{1,0:T(8,128)(2,1)S(1)} %copy-done), channel_id=1, source_target_pairs={{0,1},{1,0},{2,3},{3,2},{4,5},{5,4},{6,7},{7,6},{8,9},{9,8},{10,11... | collective-permute-start | bytes 2752520 | tf_op jit(solution)/shard_map/ppermute | solution.py:17
  91.2 13.1 %all-to-all-done = bf16[8,24,1792]{2,1,0:T(8,128)(2,1)S(1)} async-done(((bf16[8,24,1792]{2,1,0:T(8,128)(2,1)}), bf16[8,24,1792]{2,1,0:T(8,128)(2,1)S(1)}, u32[]{:S(2)}, u32[]{:S(2)}) %all-to-all-start) | async-done | bytes 688160 | tf_op jit(solution)/shard_map/all_to_all | solution.py:8
  104.3 0.1 add_bitcast_fusion
  104.5 13.8 %all_to_all.15 = bf16[8,24,896]{2,1,0:T(8,128)(2,1)S(1)} all-to-all(bf16[8,24,896]{2,1,0:T(8,128)(2,1)S(1)} %broadcast_in_dim.2), channel_id=1, replica_groups=mesh['groups'=2,'mp'=16,'dp'=8,'guide'=2] {'dp'}, dimensions={0} | all-to-all | bytes 688128 | tf_op jit(solution)/shard_map/all_to_all | solution.py:51
  118.2 0.4 convolution_convert_fusion.1
  118.6 0.0 collective-permute-done.2
  118.6 0.4 convolution_convert_fusion
  119.0 0.1 select_bitcast_fusion.1
  119.1 0.1 pad_maximum_fusion.1
  119.2 24.1 %all_to_all.16 = bf16[16,32,512]{2,1,0:T(8,128)(2,1)S(1)} all-to-all(bf16[16,32,512]{2,1,0:T(8,128)(2,1)S(1)} %bitcast.39), channel_id=1, replica_groups=mesh['groups'=2,'mp'=16,'dp'=8,'guide'=2] {'mp'}, dimensions={0} | all-to-all | bytes 1048576 | tf_op jit(solution)/shard_map/all_to_all | solution.py:8
  143.3 0.1 fusion.9
  143.4 2.0 %collective-permute-start.3 = (bf16[16,512]{1,0:T(8,128)(2,1)S(1)}, bf16[16,512]{1,0:T(8,128)(2,1)S(1)}, u32[]{:S(2)}, u32[]{:S(2)}) collective-permute-start(bf16[16,512]{1,0:T(8,128)(2,1)S(1)} %get-tuple-element.16), channel_id=1, source_target_pairs={{0,1},{1,0},{2,3},{3,2},{4,5},{5,4},{6,7},{7,6},{8,9},{9,8},{10,11... | collective-permute-start | bytes 49160 | tf_op jit(solution)/shard_map/ppermute | solution.py:17
  145.3 1.1 collective-permute-done.3
  146.5 0.6 maximum_select_fusion
  (13 shorter events, 0.2 us)
Async XLA Ops:
  0.0 3.6 %copy-start.1 = (bf16[24,512]{1,0:T(8,128)(2,1)S(1)}, bf16[24,512]{1,0:T(8,128)(2,1)}, u32[]{:S(2)}) copy-start(bf16[24,512]{1,0:T(8,128)(2,1)} %param.4) | copy-start | bytes 73732
  1.6 77.3 %collective-permute-start.1 = (bf16[512,1792]{1,0:T(8,128)(2,1)S(1)}, bf16[512,1792]{1,0:T(8,128)(2,1)}, u32[]{:S(2)}, u32[]{:S(2)}) collective-permute-start(bf16[512,1792]{1,0:T(8,128)(2,1)S(1)} %pad_maximum_fusion), channel_id=1, source_target_pairs={{0,1},{1,0},{2,3},{3,2},{4,5},{5,4},{6,7},{7,6},{8,9},{9,8},{10,11... | collective-permute-start | bytes 5505032 | tf_op jit(solution)/shard_map/ppermute | solution.py:17
  3.6 3.9 %collective-permute-start = (bf16[24,512]{1,0:T(8,128)(2,1)S(1)}, bf16[24,512]{1,0:T(8,128)(2,1)S(1)}, u32[]{:S(2)}, u32[]{:S(2)}) collective-permute-start(bf16[24,512]{1,0:T(8,128)(2,1)S(1)} %copy-done.1), channel_id=1, source_target_pairs={{0,1},{1,0},{2,3},{3,2},{4,5},{5,4},{6,7},{7,6},{8,9},{9,8},{10,11... | collective-permute-start | bytes 73736 | tf_op jit(solution)/shard_map/ppermute | solution.py:17
  78.9 10.3 %copy-start = (bf16[896,512]{1,0:T(8,128)(2,1)S(1)}, bf16[896,512]{1,0:T(8,128)(2,1)}, u32[]{:S(2)}) copy-start(bf16[896,512]{1,0:T(8,128)(2,1)} %param.7) | copy-start | bytes 2752516
  81.9 22.4 %all-to-all-start = ((bf16[8,24,1792]{2,1,0:T(8,128)(2,1)}), bf16[8,24,1792]{2,1,0:T(8,128)(2,1)S(1)}, u32[]{:S(2)}, u32[]{:S(2)}) async-start(bf16[8,24,1792]{2,1,0:T(8,128)(2,1)} %bitcast.8), calls=%async_computation | async-start | bytes 1376256 | tf_op jit(solution)/shard_map/all_to_all | solution.py:8
  89.2 29.4 %collective-permute-start.2 = (bf16[896,512]{1,0:T(8,128)(2,1)S(1)}, bf16[896,512]{1,0:T(8,128)(2,1)S(1)}, u32[]{:S(2)}, u32[]{:S(2)}) collective-permute-start(bf16[896,512]{1,0:T(8,128)(2,1)S(1)} %copy-done), channel_id=1, source_target_pairs={{0,1},{1,0},{2,3},{3,2},{4,5},{5,4},{6,7},{7,6},{8,9},{9,8},{10,11... | collective-permute-start | bytes 2752520 | tf_op jit(solution)/shard_map/ppermute | solution.py:17
  143.4 3.1 %collective-permute-start.3 = (bf16[16,512]{1,0:T(8,128)(2,1)S(1)}, bf16[16,512]{1,0:T(8,128)(2,1)S(1)}, u32[]{:S(2)}, u32[]{:S(2)}) collective-permute-start(bf16[16,512]{1,0:T(8,128)(2,1)S(1)} %get-tuple-element.16), channel_id=1, source_target_pairs={{0,1},{1,0},{2,3},{3,2},{4,5},{5,4},{6,7},{7,6},{8,9},{9,8},{10,11... | collective-permute-start | bytes 49160 | tf_op jit(solution)/shard_map/ppermute | solution.py:17
